TPU v7x, 32 devices: a whole 2x2x4 slice. The times are simulated.
32 devices in a mesh: obj: 8 (over z, x), view: 4 (over y, core).
Axes of the slice: x: 2, y: 2, z: 4, core: 2. Of those that a mesh axis runs over, the one named last changes fastest.
Arguments:
- features: bfloat16 [8, 4, 1369, 1024], P('obj', 'view'), may hold values from -6 to 6
- projection: int32 [8, 4, 1369], P('obj'), may hold values from 0 to 511, as said below
- active_count: int32 [8], P('obj'), may hold values from 256 to 512, as said below
- in_weight: bfloat16 [1024, 768], replicated, may hold values from -0.1875 to 0.1875
- norm_gain: float32 [768], replicated, may hold values from 0.1 to 1.9
- qkv_weight: bfloat16 [768, 2304], replicated, may hold values from -4 to 4
- out_weight: bfloat16 [768, 768], replicated, may hold values from -0.21875 to 0.21875
- cotangent: bfloat16 [8, 512, 768], P('obj', 'view'), may hold values from -6 to 6
Outputs:
- latent: bfloat16 [8, 512, 768], P('obj', 'view')
- in_grad: float32 [1024, 768], P('view')
- qkv_grad: float32 [768, 2304], P('view')
- out_grad: float32 [768, 768], P('view')
Inputs may be any that keep to these rules, and one draw needn't show every extreme that they name: `projection`: every entry is below its object's active_count; in every object some live slots receive no patch. `active_count`: slots from this number on are empty: they are no keys, and their rows of latent are zero.
All inputs are finite; a program needn't handle non-finite values.
Results may differ from a plain program's by a relative error of at most 0.02.
Values may be sent and summed in bfloat16 or wider, within the bound.
No kernel may reach another device: no remote copies, remote signals or barrier semaphores. Data moves between devices by JAX's collectives and lax.ppermute only.
A program may use at most 64 MiB of HBM per device.

v0:
```python
import jax
import jax.numpy as jnp
from jax import lax
from jax.sharding import PartitionSpec as P

HEAD_DIM = 64


def normalize(base_rows):
    center = jnp.mean(base_rows, axis=-1, keepdims=True)
    shifted = base_rows - center
    spread = jnp.mean(shifted * shifted, axis=-1, keepdims=True)
    inverse = lax.rsqrt(spread + 1e-06)
    return (shifted * inverse, inverse)


def per_device(
    features, projection, active_count, in_weight, norm_gain, qkv_weight, out_weight, cotangent
):
    groups = lax.axis_size("view")
    objects = lax.axis_size("obj")
    position = lax.axis_index("view")
    own_count = cotangent.shape[1]
    all_slots = own_count * groups
    width = out_weight.shape[0]
    heads = width // HEAD_DIM
    local_feat = features.reshape(features.shape[1] * features.shape[2], features.shape[3])
    local_rows = local_feat.shape[0]
    flat_proj = projection.reshape(projection.shape[1] * projection.shape[2])
    own_proj = lax.dynamic_slice_in_dim(flat_proj, position * local_rows, local_rows, 0)
    own_slots = position * own_count + lax.iota(jnp.int32, own_count)
    counts = jnp.sum((flat_proj[None, :] == own_slots[:, None]).astype(jnp.float32), axis=1)
    slot_ids = lax.iota(jnp.int32, own_count * lax.axis_size("view"))
    onehot = (own_proj[None, :] == slot_ids[:, None]).astype(jnp.bfloat16)
    totals = lax.psum_scatter(
        jnp.dot(onehot, local_feat, preferred_element_type=jnp.float32),
        "view",
        scatter_dimension=0,
        tiled=True,
    )
    voxels = (totals / jnp.maximum(counts, 1.0)[:, None]).astype(jnp.bfloat16)
    live_rows = (own_slots < active_count[0]).astype(jnp.float32)
    base_rows = jnp.dot(voxels, in_weight, preferred_element_type=jnp.float32)
    unit_rows, inverse = normalize(base_rows)
    normed = (unit_rows * norm_gain).astype(jnp.bfloat16)
    packed = jnp.dot(normed, qkv_weight, preferred_element_type=jnp.float32).astype(jnp.bfloat16)
    queries = packed[:, :width].reshape(own_count, heads, HEAD_DIM)
    key_all, value_all = (
        lax.all_gather(packed[:, width : 2 * width], "view", axis=0, tiled=True),
        lax.all_gather(packed[:, 2 * width :], "view", axis=0, tiled=True),
    )
    key_heads = key_all.reshape(all_slots, heads, HEAD_DIM)
    value_heads = value_all.reshape(all_slots, heads, HEAD_DIM)
    inv_root = HEAD_DIM ** (-0.5)
    scores = (
        jnp.einsum("qhd,khd->hqk", queries, key_heads, preferred_element_type=jnp.float32)
        * inv_root
    )
    key_live = (lax.iota(jnp.int32, all_slots) < active_count[0])[None, None, :]
    masked = jnp.where(key_live, scores, -1e30)
    row_peak = jnp.max(masked, axis=-1, keepdims=True)
    expo_terms = jnp.where(key_live, jnp.exp(masked - row_peak), 0.0)
    weights = expo_terms / jnp.sum(expo_terms, axis=-1, keepdims=True)
    prob_rows = weights.astype(jnp.bfloat16)
    mixed_full = jnp.einsum(
        "hqk,khd->qhd", prob_rows, value_heads, preferred_element_type=jnp.float32
    )
    attended = mixed_full.reshape(own_count, width).astype(jnp.bfloat16)
    branch = jnp.dot(attended, out_weight, preferred_element_type=jnp.float32)
    latent = (live_rows[:, None] * (base_rows + branch)).astype(jnp.bfloat16)
    seed_rows = (cotangent[0].astype(jnp.float32) * live_rows[:, None] * (1.0 / objects)).astype(
        jnp.bfloat16
    )
    out_term = jnp.einsum("rc,rd->cd", attended, seed_rows, preferred_element_type=jnp.float32)
    grad_attended = jnp.einsum(
        "rd,cd->rc", seed_rows, out_weight, preferred_element_type=jnp.float32
    ).astype(jnp.bfloat16)
    grad_heads = grad_attended.reshape(own_count, heads, HEAD_DIM)
    grad_probs = jnp.einsum(
        "qhd,khd->hqk", grad_heads, value_heads, preferred_element_type=jnp.float32
    )
    delta_rows = jnp.sum(grad_heads.astype(jnp.float32) * mixed_full, axis=-1).T[:, :, None]
    grad_scores = (weights * (grad_probs - delta_rows) * inv_root).astype(jnp.bfloat16)
    grad_queries = jnp.einsum(
        "hqk,khd->qhd", grad_scores, key_heads, preferred_element_type=jnp.float32
    ).reshape(own_count, width)
    key_part = jnp.einsum(
        "hqk,qhd->khd", grad_scores, queries, preferred_element_type=jnp.float32
    ).reshape(own_count * lax.axis_size("view"), width)
    value_part = jnp.einsum(
        "hqk,qhd->khd", prob_rows, grad_heads, preferred_element_type=jnp.float32
    ).reshape(own_count * lax.axis_size("view"), width)
    key_grads = lax.psum_scatter(
        jnp.concatenate([key_part, value_part], axis=1).astype(jnp.bfloat16),
        "view",
        scatter_dimension=0,
        tiled=True,
    ).astype(jnp.float32)
    grad_packed = jnp.concatenate([grad_queries, key_grads], axis=1).astype(jnp.bfloat16)
    qkv_term = jnp.einsum("rc,rd->cd", normed, grad_packed, preferred_element_type=jnp.float32)
    grad_normed = jnp.einsum(
        "rd,cd->rc", grad_packed, qkv_weight, preferred_element_type=jnp.float32
    )
    grad_unit = grad_normed * norm_gain
    grad_branch = inverse * (
        grad_unit
        - jnp.mean(grad_unit, axis=-1, keepdims=True)
        - unit_rows * jnp.mean(grad_unit * unit_rows, axis=-1, keepdims=True)
    )
    grad_base = (seed_rows.astype(jnp.float32) + grad_branch).astype(jnp.bfloat16)
    in_term = jnp.einsum("rc,rd->cd", voxels, grad_base, preferred_element_type=jnp.float32)
    in_share, qkv_share, out_share = (
        lax.psum_scatter(
            in_term.astype(jnp.bfloat16), "view", scatter_dimension=0, tiled=True
        ).astype(jnp.float32),
        lax.psum_scatter(
            qkv_term.astype(jnp.bfloat16), "view", scatter_dimension=0, tiled=True
        ).astype(jnp.float32),
        lax.psum_scatter(
            out_term.astype(jnp.bfloat16), "view", scatter_dimension=0, tiled=True
        ).astype(jnp.float32),
    )
    in_grad, qkv_grad, out_grad = (
        lax.psum(in_share.astype(jnp.bfloat16), "obj").astype(jnp.float32),
        lax.psum(qkv_share.astype(jnp.bfloat16), "obj").astype(jnp.float32),
        lax.psum(out_share.astype(jnp.bfloat16), "obj").astype(jnp.float32),
    )
    return (latent[None], in_grad, qkv_grad, out_grad)


def solution(mesh):
    return jax.shard_map(
        per_device,
        mesh=mesh,
        in_specs=(
            P("obj", "view", None, None),
            P("obj", None, None),
            P("obj"),
            P(),
            P(),
            P(),
            P(),
            P("obj", "view", None),
        ),
        out_specs=(P("obj", "view", None), P("view", None), P("view", None), P("view", None)),
        check_vma=False,
    )
```

profile of v0, /device:TPU:0, one launch (start us, length us, event | category | flops | bytes accessed | tf_op | source)
XLA Modules:
  0.0 329.2 jit_solution(13558839476085592983)
XLA Ops:
  9.6 4.9 %fusion.1 = f32[512,1024]{1,0:T(8,128)} fusion(bf16[1,1,1369,1024]{3,2,1,0:T(8,128)(2,1)} %param.8, s32[1369]{0:T(1024)S(1)} %dynamic_slice.3), kind=kOutput, calls=%fused_computation.7 | convolution fusion | flops 1436201472 | bytes 4906340 | tf_op jit(solution)/shard_map/dot_general | solution.py:36
  15.8 2.6 convolution_convert_fusion.7
  20.7 3.0 convert_reduce_fusion
  23.8 24.8 %reduce-scatter.8.cloned.1.call-done = f32[128,1024]{1,0:T(8,128)} async-done(((f32[512,1024]{1,0:T(8,128)}), f32[128,1024]{1,0:T(8,128)}) %reduce-scatter.8.cloned.1.call-update) | async-done | bytes 524304 | tf_op jit(solution)/shard_map/reduce_scatter | solution.py:35
  48.6 2.1 fusion.39
  54.2 9.0 %all_gather.7 = bf16[512,768]{1,0:T(8,128)(2,1)} all-gather(bf16[128,768]{1,0:T(8,128)(2,1)} %get-tuple-element.9), channel_id=1, replica_groups=mesh['obj'=8,'view'=4] {'view'}, dimensions={0}, use_global_device_ids=true | all-gather | bytes 983040 | tf_op jit(solution)/shard_map/all_gather | solution.py:49
  63.3 2.3 copy.29
  65.6 10.7 %all_gather.6 = bf16[512,768]{1,0:T(8,128)(2,1)} all-gather(bf16[128,768]{1,0:T(8,128)(2,1)} %get-tuple-element.11), channel_id=1, replica_groups=mesh['obj'=8,'view'=4] {'view'}, dimensions={0}, use_global_device_ids=true | all-gather | bytes 983040 | tf_op jit(solution)/shard_map/all_gather | solution.py:50
  76.3 2.3 copy.27
  78.6 4.1 %fusion.40 = (f32[12,128]{1,0:T(8,128)S(1)}, f32[12,128,512]{2,1,0:T(8,128)}) fusion(pred[512]{0:T(512)(128)(4,1)} %iota_compare_fusion.2, bf16[128,12,64]{0,2,1:T(8,128)(2,1)} %bitcast.75, bf16[512,12,64]{0,2,1:T(8,128)(2,1)} %bitcast.62), kind=kOutput, calls=%fused_computation.72 | convolution fusion | flops 104595968 | bytes 4135424 | tf_op jit(solution)/shard_map/sub | solution.py:62
  82.6 2.2 fusion.8
  91.1 2.6 copy.31
  93.8 2.6 convolution_convert_fusion.3
  96.5 3.0 convolution_convert_fusion.6
  99.4 22.5 %reduce-scatter.16.cloned.1.call-done = bf16[128,1536]{1,0:T(8,128)(2,1)} async-done(((bf16[512,1536]{1,0:T(8,128)(2,1)}), bf16[128,1536]{1,0:T(8,128)(2,1)}) %reduce-scatter.16.cloned.1.call-update) | async-done | bytes 393232
  123.9 2.7 fusion.37
  126.6 1.9 convolution_convert_fusion.2
  128.6 4.1 %convolution_convert_fusion = bf16[768,2304]{1,0:T(8,128)(2,1)} fusion(bf16[128,1536]{0,1:T(8,128)(2,1)} %copy.32, bf16[128,768]{0,1:T(8,128)(2,1)} %bitcast.69, f32[128,768]{1,0:T(8,128)} %copy-done.1, f32[768]{0:T(1024)S(1)} %copy-done.10, f32[128]{0:T(128)S(1)} %copy-done.14, f32[128]{0:T(128)S(1)} %broadcast_multiply_fusion.2), kind=kOutput, calls=%fused_computation.1 | convolution fusion | flops 456327168 | bytes 4526080 | tf_op jit(solution)/shard_map/rc,rd->cd/dot_general | solution.py:100
  132.8 17.3 %reduce-scatter.14.cloned.1.call-done = bf16[192,768]{1,0:T(8,128)(2,1)} async-done(((bf16[768,768]{1,0:T(8,128)(2,1)}), bf16[192,768]{1,0:T(8,128)(2,1)}) %reduce-scatter.14.cloned.1.call-update) | async-done | bytes 294928 | tf_op jit(solution)/shard_map/reduce_scatter | solution.py:119
  150.1 31.0 %reduce-scatter.10.cloned.1.call-done = bf16[256,768]{1,0:T(8,128)(2,1)} async-done(((bf16[1024,768]{1,0:T(8,128)(2,1)}), bf16[256,768]{1,0:T(8,128)(2,1)}) %reduce-scatter.10.cloned.1.call-update) | async-done | bytes 393232 | tf_op jit(solution)/shard_map/reduce_scatter | solution.py:113
  181.2 42.8 %reduce-scatter.12.cloned.1.call-done = bf16[192,2304]{1,0:T(8,128)(2,1)} async-done(((bf16[768,2304]{1,0:T(8,128)(2,1)}), bf16[192,2304]{1,0:T(8,128)(2,1)}) %reduce-scatter.12.cloned.1.call-update) | async-done | bytes 884752 | tf_op jit(solution)/shard_map/reduce_scatter | solution.py:116
  224.0 2.4 fusion.11
  226.5 90.8 %all-reduce.3.cloned.1.call-done = (bf16[256,768]{1,0:T(8,128)(2,1)}, bf16[192,2304]{1,0:T(8,128)(2,1)}, bf16[192,768]{1,0:T(8,128)(2,1)}) async-done(((bf16[256,768]{1,0:T(8,128)(2,1)}, bf16[192,2304]{1,0:T(8,128)(2,1)}, bf16[192,768]{1,0:T(8,128)(2,1)}), (bf16[256,768]{1,0:T(8,128)(2,1)}, bf16[192,2304]{1,0:T(8,128)(2,1)}, bf16[192,768]{1,0:T(8,128)(2,1)})) %all-reduce.3.cloned.1.call-update) | async-done | bytes 1572880 | tf_op jit(solution)/shard_map/psum | solution.py:124
  317.2 2.0 convert_element_type.110
  (70 shorter events, 20.3 us)
Async XLA Ops:
  7.2 43.7 %copy-start = (bf16[768,2304]{1,0:T(8,128)(2,1)S(1)}, bf16[768,2304]{1,0:T(8,128)(2,1)}, u32[]{:S(2)}) copy-start(bf16[768,2304]{1,0:T(8,128)(2,1)} %param.13) | copy-start | bytes 10616836
  7.2 41.4 %reduce-scatter.8.cloned.1.call-start = ((), (), s32[]{:S(2)}) async-start(), calls=%async_computation.5 | async-start | bytes 2621440 | tf_op jit(solution)/shard_map/reduce_scatter | solution.py:35
  14.5 107.4 %reduce-scatter.16.cloned.1.call-start = ((), (), s32[]{:S(2)}) async-start(), calls=%async_computation.9 | async-start | bytes 1966080
  15.2 0.6 copy-start.11
  18.4 32.5 %copy-start.10 = (f32[768]{0:T(1024)S(1)}, f32[768]{0:T(1024)}, u32[]{:S(2)}) copy-start(f32[768]{0:T(1024)} %param.12) | copy-start | bytes 9220
  23.8 26.9 %copy-start.16 = (f32[128]{0:T(128)}, f32[128]{0:T(128)S(1)}, u32[]{:S(2)}) copy-start(f32[128]{0:T(128)S(1)} %broadcast_maximum_fusion) | copy-start | bytes 1540
  50.7 1.0 copy-start.1
  50.9 1.6 copy-start.13
  82.6 2.2 copy-start.6
  84.9 1.1 copy-start.5
  84.9 2.5 copy-start.4
  87.4 2.2 copy-start.8
  88.3 1.2 copy-start.3
  91.1 2.7 copy-start.12
  93.7 56.4 %reduce-scatter.14.cloned.1.call-start = ((), (), s32[]{:S(2)}) async-start(), calls=%async_computation.8 | async-start | bytes 1474560 | tf_op jit(solution)/shard_map/reduce_scatter | solution.py:119
  96.4 27.5 %copy-start.14 = (f32[128]{0:T(128)S(1)}, f32[128]{0:T(128)}, u32[]{:S(2)}) copy-start(f32[128]{0:T(128)} %copy-done.13) | copy-start | bytes 1540
  96.4 84.8 %reduce-scatter.10.cloned.1.call-start = ((), (), s32[]{:S(2)}) async-start(), calls=%async_computation.6 | async-start | bytes 1966080 | tf_op jit(solution)/shard_map/reduce_scatter | solution.py:113
  123.8 2.7 copy-start.2
  123.8 2.7 copy-start.9
  123.8 2.7 copy-start.15
  123.8 2.8 copy-start.17
  128.5 95.4 %reduce-scatter.12.cloned.1.call-start = ((), (), s32[]{:S(2)}) async-start(), calls=%async_computation.7 | async-start | bytes 4423680 | tf_op jit(solution)/shard_map/reduce_scatter | solution.py:116
  132.7 184.5 %all-reduce.3.cloned.1.call-start = ((), (), s32[]{:S(2)}) async-start(), calls=%async_computation.10 | async-start | bytes 3145728 | tf_op jit(solution)/shard_map/psum | solution.py:124
  317.2 3.8 %copy-start.7 = (bf16[192,2304]{1,0:T(8,128)(2,1)S(1)}, bf16[192,2304]{1,0:T(8,128)(2,1)}, u32[]{:S(2)}) copy-start(bf16[192,2304]{1,0:T(8,128)(2,1)} %get-tuple-element.7) | copy-start | bytes 2654212
Sparse Core Ops, SparseCore 0:
  14.7 33.8 reduce-scatter.7
  93.9 28.0 reduce-scatter.15
  124.5 25.6 reduce-scatter.13
  153.1 28.0 reduce-scatter.9
  183.6 40.3 reduce-scatter.11
  227.6 89.5 all-reduce.2
where the time goes:
time: 330 us; the launch traced here: 329 us
  waiting for transfers between devices  229 us (69%)
  matrix products  34.1 us (10%)
  blocking collectives  19.8 us (6%)
  local copies, waits for them, and re-layouts  18.3 us (6%)
  between operations  15 us (5%)
  other arithmetic  12.4 us (4%)
    psum x1, waiting for transfers between devices, per_device(): lax.psum(in_share.astype(jnp.bfloat16), 'obj').astype(jnp.float32)  90.8 us
    reduce_scatter x1, waiting for transfers between devices, per_device(): lax.psum_scatter(qkv_term.astype(jnp.bfloat16), 'view', scatter_dimension...  42.8 us
    reduce_scatter x1, waiting for transfers between devices, per_device(): lax.psum_scatter(in_term.astype(jnp.bfloat16), 'view', scatter_dimension=...  31 us
    reduce_scatter x1, waiting for transfers between devices, per_device(): lax.psum_scatter(jnp.dot(onehot, local_feat, preferred_element_type=jnp.f...  24.8 us
    unnamed x7, waiting for transfers between devices  22.6 us
    reduce_scatter x1, waiting for transfers between devices, per_device(): lax.psum_scatter(out_term.astype(jnp.bfloat16), 'view', scatter_dimension...  17.3 us
    all_gather x1, blocking collectives, per_device(): lax.all_gather(packed[:, 2 * width:], 'view', axis=0, tiled=True)  10.7 us
    all_gather x1, blocking collectives, per_device(): lax.all_gather(packed[:, width:2 * width], 'view', axis=0, tiled=True)  9.05 us
  transfers between devices with their start and end apart: 6, of which 6 were waited for; matrix products, arithmetic and copies ran while one was open for 8% of the time, Pallas kernels for 0%

commit v1 on v0

v1 whole, which is shorter than its diff:
```python
import jax
import jax.numpy as jnp
from jax import lax
from jax.experimental import pallas as pl
from jax.experimental.pallas import tpu as pltpu
from jax.sharding import PartitionSpec as P

HEAD_DIM = 64
F32 = jnp.float32
BF16 = jnp.bfloat16
VMEM_LIMIT = 60 * 1024 * 1024

NN = (((1,), (0,)), ((), ()))
NT = (((1,), (1,)), ((), ()))
TN = (((0,), (0,)), ((), ()))


def dot(lhs, rhs, dims):
    return lax.dot_general(lhs, rhs, dims, preferred_element_type=F32)


def vmem_call(body, out_shape, scalars, arrays, scratch=()):
    return pl.pallas_call(
        body,
        out_shape=out_shape,
        in_specs=[pl.BlockSpec(memory_space=pltpu.SMEM)] * len(scalars)
        + [pl.BlockSpec(memory_space=pltpu.VMEM)] * len(arrays),
        out_specs=jax.tree.map(lambda _: pl.BlockSpec(memory_space=pltpu.VMEM), out_shape),
        scratch_shapes=scratch,
        compiler_params=pltpu.CompilerParams(vmem_limit_bytes=VMEM_LIMIT),
    )(*scalars, *arrays)


def exchange(value, axis, mask):
    size = lax.axis_size(axis)
    return lax.ppermute(value, axis, [(i, i ^ mask) for i in range(size)])


def bit_masks(size):
    bits = size.bit_length() - 1
    masks = [1 << b for b in range(bits)]
    if bits >= 3:
        masks[2] = 6
    return masks


def keep_bit(index, masks, which):
    mask = masks[which]
    if mask == 2 and 6 in masks:
        return ((index >> 1) ^ (index >> 2)) & 1
    top = mask.bit_length() - 1
    return (index >> top) & 1


def totals_body(block, core_ref, proj_ref, feat_ref, own_ref, send_ref):
    core = core_ref[0]
    rows = own_ref.shape[0]
    row = lax.broadcasted_iota(jnp.int32, (rows, 1), 0)
    for half, ref in ((1 - core, send_ref), (core, own_ref)):
        ids = ((row // block) * 2 + half) * block + row % block
        onehot = jnp.where(proj_ref[...] == ids, 1.0, 0.0).astype(BF16)
        ref[...] = dot(onehot, feat_ref[...], NN).astype(ref.dtype)


def counts_body(block, core_ref, proj_ref, inv_ref):
    core = core_ref[0]
    rows = inv_ref.shape[0]
    row = lax.broadcasted_iota(jnp.int32, (rows, 1), 0)
    ids = ((row // block) * 2 + core) * block + row % block
    onehot = jnp.where(proj_ref[...] == ids, 1.0, 0.0)
    inv_ref[...] = jnp.maximum(jnp.sum(onehot, axis=1, keepdims=True), 1.0)


def attend_body(
    block, core_ref, active_ref, own_ref, other_ref, in_wt_ref, wt_ref, gain_ref, douts_ref,
    gp_ref, att_ref, unit_ref, inv_ref, normed_ref, vox_ref, packed_ref
):
    core = core_ref[0]
    half = own_ref.shape[0]
    slots = 2 * half
    heads_rows = att_ref.shape[0]
    heads = heads_rows // HEAD_DIM
    own_at = pl.multiple_of(core * half, half)
    other_at = pl.multiple_of((1 - core) * half, half)
    vox_ref[pl.ds(own_at, half), :] = own_ref[...]
    vox_ref[pl.ds(other_at, half), :] = other_ref[...]
    base = dot(in_wt_ref[...], vox_ref[...], NT)
    width = base.shape[0]
    center = jnp.sum(base, axis=0, keepdims=True) * (1.0 / width)
    shifted = base - center
    spread = jnp.sum(shifted * shifted, axis=0, keepdims=True) * (1.0 / width)
    inverse = lax.rsqrt(spread + 1e-06)
    unit = shifted * inverse
    inv_ref[...] = inverse
    unit_ref[...] = unit
    normed_ref[...] = (unit * gain_ref[...]).astype(BF16)
    packed_ref[...] = dot(wt_ref[...], normed_ref[...], NN).astype(BF16)
    row = lax.broadcasted_iota(jnp.int32, (slots, 1), 0)
    local = row % half
    ids = ((local // block) * 2 + row // half) * block + local % block
    live = ids < active_ref[0]

    @pl.loop(0, heads)
    def _(head):
        at = pl.multiple_of(head * HEAD_DIM, HEAD_DIM)
        query = packed_ref[pl.ds(at, HEAD_DIM), :] * BF16(HEAD_DIM**-0.5)
        key = packed_ref[pl.ds(heads_rows + at, HEAD_DIM), :]
        value = packed_ref[pl.ds(2 * heads_rows + at, HEAD_DIM), :]
        dout = douts_ref[pl.ds(at, HEAD_DIM), :]
        scores = jnp.where(live, dot(key, query, TN), -1e30)
        peak = jnp.max(scores, axis=0, keepdims=True)
        expo = jnp.exp(scores - peak)
        weights = expo * (1.0 / jnp.sum(expo, axis=0, keepdims=True))
        probs = weights.astype(BF16)
        mixed = dot(value, probs, NN)
        att_ref[pl.ds(at, HEAD_DIM), :] = mixed.astype(BF16)
        gp_ref[pl.ds(2 * heads_rows + at, HEAD_DIM), :] = dot(dout, probs, NT).astype(BF16)
        delta = jnp.sum(dout.astype(F32) * mixed, axis=0, keepdims=True)
        grad = (weights * (dot(value, dout, TN) - delta)).astype(BF16)
        grad_query = dot(key, grad, NN) * HEAD_DIM**-0.5
        gp_ref[pl.ds(at, HEAD_DIM), :] = grad_query.astype(BF16)
        gp_ref[pl.ds(heads_rows + at, HEAD_DIM), :] = dot(query, grad, NT).astype(BF16)


def write_pieces(value, scratch_ref, flips, keep_ref, send_ref):
    scratch_ref[...] = value
    rows = scratch_ref.shape[0] // 4
    for piece in range(4):
        source = pl.multiple_of((flips ^ piece) * rows, 8)
        block = scratch_ref[pl.ds(source, rows), :]
        ref = send_ref if piece >= 2 else keep_ref
        ref[piece % 2] = block.astype(ref.dtype)


def own_grads_body(
    share_ref, flip_ref, normed_ref, gp_ref, att_ref, seed_ref, keep_ref, send_ref, acc_ref
):
    rows = acc_ref.shape[0]
    normed = normed_ref[pl.ds(pl.multiple_of(share_ref[0] * rows, 16), rows), :]
    value = jnp.concatenate(
        [dot(normed, gp_ref[...], NT), dot(att_ref[...], seed_ref[...], NN)], axis=1
    )
    write_pieces(value, acc_ref, flip_ref[0], keep_ref, send_ref)


def in_grad_body(
    flip_ref, gp_own_ref, gp_other_ref, w_own_ref, w_other_ref, unit_ref, inv_ref, gain_ref,
    seed_ref, vox_ref, keep_ref, send_ref, acc_ref
):
    grad_normed = dot(w_own_ref[...], gp_own_ref[...], NN) + dot(
        w_other_ref[...], gp_other_ref[...], NN
    )
    unit = unit_ref[...]
    width = unit.shape[0]
    grad_unit = grad_normed * gain_ref[...]
    mean_one = jnp.sum(grad_unit, axis=0, keepdims=True) * (1.0 / width)
    mean_two = jnp.sum(grad_unit * unit, axis=0, keepdims=True) * (1.0 / width)
    branch = inv_ref[...] * (grad_unit - mean_one - unit * mean_two)
    grad_base = (seed_ref[...].astype(F32) + branch).astype(BF16)
    write_pieces(dot(vox_ref[...], grad_base, NT), acc_ref, flip_ref[0], keep_ref, send_ref)


def assemble_body(
    core_ref, fa_ref, fb_ref, fc_ref, a0, a1, a2, b0, b1, b2, c0, c1, c2,
    in_ref, qkv_ref, out_ref
):
    core = core_ref[0]
    width = out_ref.shape[1]
    part = width // 2
    rows = a0.shape[0]
    for flips, half, pieces in ((fa_ref[0], core, (a0, a1, a2)), (fb_ref[0], 1 - core, (b0, b1, b2))):
        first, second, rest = pieces
        for piece in range(4):
            source = (first, second)[piece] if piece < 2 else rest.at[piece - 2]
            block = source[...].astype(F32)
            to = pl.multiple_of((flips ^ piece) * rows, 8)
            for third in range(3):
                column = pl.multiple_of(third * width + half * part, 128)
                qkv_ref[pl.ds(to, rows), pl.ds(column, part)] = block[:, third * part : third * part + part]
            side = 0 if first is a0 else part
            out_ref[pl.ds(to, rows), side : side + part] = block[:, 3 * part :]
    rows = c0.shape[0]
    for piece in range(4):
        source = (c0, c1)[piece] if piece < 2 else c2.at[piece - 2]
        to = pl.multiple_of((fc_ref[0] ^ piece) * rows, 8)
        in_ref[pl.ds(to, rows), :] = source[...].astype(F32)


def reduce_steps(streams, masks):
    keeps, sends, orders = zip(*streams)
    count = len(streams)
    got = [exchange(s, "obj", masks[o[0]]) for s, o in zip(sends, orders)]
    halves = [k + g.astype(F32) for k, g in zip(keeps, got)]
    got = [exchange(h[1].astype(BF16), "obj", masks[o[1]]) for h, o in zip(halves, orders)]
    parts = [h[0] + g.astype(F32) for h, g in zip(halves, got)]
    for step in range(2, len(masks)):
        parts = [p.astype(BF16) for p in parts]
        got = [exchange(p, "obj", masks[o[step]]) for p, o in zip(parts, orders)]
        parts = [p.astype(F32) + g.astype(F32) for p, g in zip(parts, got)]
    parts = [p.astype(BF16) for p in parts]
    seconds = [exchange(p, "obj", masks[o[1]]) for p, o in zip(parts, orders)]
    rests = [
        exchange(jnp.stack([p, s]), "obj", masks[o[0]]) for p, s, o in zip(parts, seconds, orders)
    ]
    return [(parts[i], seconds[i], rests[i]) for i in range(count)]


def per_device(
    features, projection, active_count, in_weight, norm_gain, qkv_weight, out_weight, cotangent
):
    groups = lax.axis_size("view")
    objects = lax.axis_size("obj")
    view = lax.axis_index("view")
    obj = lax.axis_index("obj")
    core = view % 2
    core_s = core[None]
    block = cotangent.shape[1]
    slots = block * groups
    half = slots // 2
    feat = in_weight.shape[0]
    width = out_weight.shape[0]
    part = width // 2
    share = width // groups
    share_in = feat // groups

    rows = cotangent[0]
    mask = 2
    stack = rows[None]
    while mask < groups:
        got = exchange(stack, "view", mask)
        low = (view & mask) == 0
        stack = jnp.concatenate([jnp.where(low, stack, got), jnp.where(low, got, stack)])
        mask *= 2
    rows = stack.reshape(half, width)
    got = exchange(rows, "view", 1)
    cot = jnp.concatenate([jnp.where(core == 0, rows, got), jnp.where(core == 0, got, rows)])
    slot = lax.iota(jnp.int32, slots)
    slot_ids = ((slot % half // block) * 2 + slot // half) * block + slot % block
    live = (slot_ids < active_count[0]).astype(F32)
    seed = (cot.astype(F32) * live[:, None] * (1.0 / objects)).astype(BF16)
    seed_t = seed.T

    local_feat = features.reshape(features.shape[1] * features.shape[2], feat)
    flat_proj = projection.reshape(1, projection.shape[1] * projection.shape[2])
    local_rows = local_feat.shape[0]
    own_proj = lax.dynamic_slice_in_dim(flat_proj, view * local_rows, local_rows, 1)
    own, send = vmem_call(
        lambda *refs: totals_body(block, *refs),
        (jax.ShapeDtypeStruct((half, feat), F32), jax.ShapeDtypeStruct((half, feat), BF16)),
        (core_s,),
        (own_proj, local_feat),
    )
    total = own + exchange(send, "view", 1).astype(F32)
    mask = 2
    while mask < groups:
        total = total + exchange(total.astype(BF16), "view", mask).astype(F32)
        mask *= 2
    counts = vmem_call(
        lambda *refs: counts_body(block, *refs),
        jax.ShapeDtypeStruct((half, 1), F32),
        (core_s,),
        (flat_proj,),
    )
    vox_own = (total / counts).astype(BF16)
    vox_other = exchange(vox_own, "view", 1)

    def columns(which):
        return jnp.concatenate(
            [
                lax.dynamic_slice_in_dim(qkv_weight, t * width + which * part, part, 1)
                for t in range(3)
            ],
            axis=1,
        )

    w_own, w_other = columns(core), columns(1 - core)
    out_rows = lax.dynamic_slice_in_dim(out_weight, core * part, part, 0)
    douts = dot(out_rows, seed, NT).astype(BF16)
    gain = norm_gain[:, None]

    gp_own, att_own, unit, inverse, normed = vmem_call(
        lambda *refs: attend_body(block, *refs),
        (
            jax.ShapeDtypeStruct((3 * part, slots), BF16),
            jax.ShapeDtypeStruct((part, slots), BF16),
            jax.ShapeDtypeStruct((width, slots), F32),
            jax.ShapeDtypeStruct((1, slots), F32),
            jax.ShapeDtypeStruct((width, slots), BF16),
        ),
        (core_s, active_count),
        (vox_own, vox_other, in_weight.T, w_own.T, gain, douts),
        [pltpu.VMEM((slots, feat), BF16), pltpu.VMEM((3 * part, slots), BF16)],
    )
    att_other = exchange(att_own, "view", 1)
    gp_other = exchange(gp_own, "view", 1)

    masks = bit_masks(objects)
    orders = [[(s + j) % len(masks) for j in range(len(masks))] for s in (0, 1, 2)]
    flips = [
        (keep_bit(obj, masks, o[0]) * 2 + keep_bit(obj, masks, o[1])).astype(jnp.int32)[None]
        for o in orders
    ]
    att = jnp.where(core == 0, jnp.stack([att_own, att_other]), jnp.stack([att_other, att_own]))
    att_share = lax.dynamic_slice_in_dim(att.reshape(width, slots), view * share, share, 0)
    vox = jnp.where(core == 0, jnp.stack([vox_own, vox_other]), jnp.stack([vox_other, vox_own]))
    vox_share = lax.dynamic_slice_in_dim(vox.reshape(slots, feat), view * share_in, share_in, 1).T

    def pieces(r, c):
        return (
            jax.ShapeDtypeStruct((2, r // 4, c), F32),
            jax.ShapeDtypeStruct((2, r // 4, c), BF16),
        )

    def half_grads(gp, seed_cols, flip):
        return vmem_call(
            own_grads_body,
            pieces(share, 2 * width),
            (view[None], flip),
            (normed, gp, att_share, seed_cols),
            [pltpu.VMEM((share, 2 * width), F32)],
        )

    first = half_grads(gp_own, seed[:, :part], flips[0])
    second = half_grads(gp_other, seed[:, part:], flips[1])
    third = vmem_call(
        in_grad_body,
        pieces(share_in, width),
        (flips[2],),
        (gp_own, gp_other, w_own, w_other, unit, inverse, gain, seed_t, vox_share),
        [pltpu.VMEM((share_in, width), F32)],
    )
    sums = reduce_steps(
        [(*first, orders[0]), (*second, orders[1]), (*third, orders[2])], masks
    )
    in_grad, qkv_grad, out_grad = vmem_call(
        assemble_body,
        (
            jax.ShapeDtypeStruct((share_in, width), F32),
            jax.ShapeDtypeStruct((share, 3 * width), F32),
            jax.ShapeDtypeStruct((share, width), F32),
        ),
        (core_s, *flips),
        tuple(x for s in sums for x in s),
    )

    chip = view // 2
    vox_rows = lax.dynamic_slice_in_dim(vox_own, chip * block, block, 0)
    att_cols = lax.dynamic_slice_in_dim(
        att.reshape(width, slots), core * half + chip * block, block, 1
    )
    latent = dot(vox_rows, in_weight, NN) + dot(att_cols, out_weight, TN)
    own_ids = view * block + lax.iota(jnp.int32, block)
    live_rows = (own_ids < active_count[0]).astype(F32)
    latent = (live_rows[:, None] * latent).astype(BF16)
    return (latent[None], in_grad, qkv_grad, out_grad)


def solution(mesh):
    return jax.shard_map(
        per_device,
        mesh=mesh,
        in_specs=(
            P("obj", "view", None, None),
            P("obj", None, None),
            P("obj"),
            P(),
            P(),
            P(),
            P(),
            P("obj", "view", None),
        ),
        out_specs=(P("obj", "view", None), P("view", None), P("view", None), P("view", None)),
        check_vma=False,
    )
```

time: 330 us -> 139 us (0.42)
  waiting for transfers between devices: 229 us -> 31.9 us
  Pallas kernels: 0 us -> 38.2 us
  matrix products: 34.1 us -> 3.57 us
  starting transfers between devices: 0.25 us -> 25.7 us
  blocking collectives: 19.8 us -> 0 us
  between operations: 15 us -> 1.66 us
  local copies, waits for them, and re-layouts: 18.3 us -> 22.2 us
    reduce_scatter x4 -> x0, waiting for transfers between devices: 116 us -> none  [the longest x1 42.8 us: per_device(): lax.psum_scatter(qkv_term.astype(jnp.bfloat16), 'view', scatter_dimension...]
    psum x1 -> x0, waiting for transfers between devices: 90.8 us -> none  [per_device(): lax.psum(in_share.astype(jnp.bfloat16), 'obj').astype(jnp.float32)]
    pallas_call x0 -> x7, Pallas kernels: none -> 38.2 us  [vmem_call(): pl.pallas_call(body, out_shape=out_shape, in_specs=[pl.BlockSpec(memory_s...]
    ppermute x0 -> x22, waiting for transfers between devices: none -> 31.9 us  [exchange(): return lax.ppermute(value, axis, [(i, i ^ mask) for i in range(size)])]
    dot_general x14 -> x3, matrix products: 30.1 us -> 3.57 us  [dot(): return lax.dot_general(lhs, rhs, dims, preferred_element_type=F32)]
    ppermute x0 -> x22, starting transfers between devices: none -> 25.7 us  [exchange(): return lax.ppermute(value, axis, [(i, i ^ mask) for i in range(size)])]
    unnamed x7 -> x0, waiting for transfers between devices: 22.6 us -> none
    all_gather x2 -> x0, blocking collectives: 19.8 us -> none  [the longest x1 10.7 us: per_device(): lax.all_gather(packed[:, 2 * width:], 'view', axis=0, tiled=True)]
  transfers between devices with their start and end apart: 6 -> 22, of which waited for: 6 -> 9; matrix products, arithmetic and copies ran while one was open for 8% -> 25% of each run, Pallas kernels for 0% -> 9%
where the time goes in v1:
time: 139 us; the launch traced here: 138 us
  Pallas kernels  38.2 us (27%)
  waiting for transfers between devices  31.9 us (23%)
  starting transfers between devices  25.7 us (18%)
  local copies, waits for them, and re-layouts  22.2 us (16%)
  other arithmetic  14.7 us (11%)
  matrix products  3.57 us (3%)
  between operations  1.66 us (1%)
    pallas_call x7, Pallas kernels, vmem_call(): pl.pallas_call(body, out_shape=out_shape, in_specs=[pl.BlockSpec(memory_s...  38.2 us
    ppermute x22, waiting for transfers between devices, exchange(): return lax.ppermute(value, axis, [(i, i ^ mask) for i in range(size)])  31.9 us
    ppermute x22, starting transfers between devices, exchange(): return lax.ppermute(value, axis, [(i, i ^ mask) for i in range(size)])  25.7 us
    unnamed x64, local copies, waits for them, and re-layouts  5.96 us
    dot_general x3, matrix products, dot(): return lax.dot_general(lhs, rhs, dims, preferred_element_type=F32)  3.57 us
    dynamic_slice x1, local copies, waits for them, and re-layouts, columns(): lax.dynamic_slice_in_dim(qkv_weight, t * width + which * part, part, 1)  3.45 us
    add x3, other arithmetic, reduce_steps(): halves = [k + g.astype(F32) for k, g in zip(keeps, got)]  3.13 us
    concatenate x2, other arithmetic, columns(): jnp.concatenate([lax.dynamic_slice_in_dim(qkv_weight, t * width + which *...  2.88 us
  transfers between devices with their start and end apart: 22, of which 9 were waited for; matrix products, arithmetic and copies ran while one was open for 25% of the time, Pallas kernels for 9%

profile of v1, /device:TPU:0, one launch (start us, length us, event | category | flops | bytes accessed | tf_op | source)
XLA Modules:
  0.0 138.0 jit_solution(9646307526654584593)
XLA Ops:
  2.3 4.6 %shard_map.111 = (f32[256,1024]{1,0:T(8,128)}, bf16[256,1024]{1,0:T(8,128)(2,1)}) custom-call(s32[1]{0:T(128)} %bitcast.1.refs_0_.core_ref, s32[1,1369]{1,0:T(1,128)} %constant_dynamic-slice_fusion.8.refs_1_, bf16[1369,1024]{1,0:T(8,128)(2,1)} %bitcast.59), custom_call_target="tpu_custom_call" | custom-call | tf_op jit(solution)/shard_map/pallas_call | solution.py:23
  7.4 2.6 %collective-permute-start.3 = (bf16[1,128,768]{2,1,0:T(8,128)(2,1)}, bf16[1,128,768]{2,1,0:T(8,128)(2,1)}, u32[]{:S(2)}, u32[]{:S(2)}) collective-permute-start(bf16[1,128,768]{2,1,0:T(8,128)(2,1)} %param.15), channel_id=1, source_target_pairs={{0,2},{1,3},{2,0},{3,1},{4,6},{5,7},{6,4},{7,5},{8,10},{9,11},{10,... | collective-permute-start | bytes 589832 | tf_op jit(solution)/shard_map/ppermute | solution.py:36
  9.9 3.5 %constant_dynamic-slice_fusion.3 = (bf16[768,384]{1,0:T(8,128)(2,1)S(1)}, bf16[768,384]{1,0:T(8,128)(2,1)S(1)}, bf16[768,384]{1,0:T(8,128)(2,1)S(1)}, bf16[768,3...) fusion(bf16[768,2304]{1,0:T(8,128)(2,1)} %param.13, s32[]{:T(128)S(6)} %select_n.152, ...), kind=kLoop, calls=%fused_computation.66 | loop fusion | bytes 7077912 | tf_op jit(solution)/shard_map/dynamic_slice | solution.py:270
  15.9 2.1 %shard_map.112 = f32[256,1]{1,0:T(8,128)} custom-call(s32[1]{0:T(128)} %bitcast.1.refs_0_.core_ref, s32[1,5476]{1,0:T(1,128)} %copy-done.28), custom_call_target="tpu_custom_call" | custom-call | tf_op jit(solution)/shard_map/pallas_call | solution.py:23
  18.0 2.3 %copy.20.refs_5_ = bf16[1152,768]{1,0:T(8,128)(2,1)} copy(bf16[1152,768]{0,1:T(8,128)(2,1)S(1)} %get-tuple-element.43) | data formatting | bytes 3538944 | tf_op jit(solution)/shard_map/transpose | solution.py:291
  21.8 2.6 %copy.18 = bf16[1024,768]{0,1:T(8,128)(2,1)} copy(bf16[1024,768]{1,0:T(8,128)(2,1)} %param.11) | data formatting | bytes 3145728 | tf_op args[3]
  32.8 14.3 %shard_map.113 = (bf16[1152,512]{1,0:T(8,128)(2,1)}, bf16[384,512]{1,0:T(8,128)(2,1)}, f32[768,512]{1,0:T(8,128)}, f32[1,512]{1,0:T(1,128)}, bf16[768,512]{1,0:T(8,128)(2,1)}) custom-call(s32[1]{0:T(128)} %bitcast.1.refs_0_.core_ref, s32[1]{0:T(128)} %copy.29.refs_1_, bf16[256,1024]{1,0:T(8,128)(2,1)} %copy-done.2, bf16[256,1024]{1,0:T(8,128)(2,1)} %copy-done.12, ...), custom_call_target="tpu_custom_call" | custom-call | tf_op jit(solution)/shard_map/pallas_call | solution.py:23
  52.0 3.3 %shard_map.114 = (f32[2,48,1536]{2,1,0:T(8,128)}, bf16[2,48,1536]{2,1,0:T(8,128)(2,1)}) custom-call(s32[1]{0:T(128)} %bitcast.13.share_ref, s32[1]{0:T(128)} %bitcast.10.flip_ref.fa_ref, bf16[768,512]{1,0:T(8,128)(2,1)} %get-tuple-element.23.normed_ref, bf16[1152,512]{1,0:T(8,128)(2,1)} %get-tuple-element.24.gp_ref.gp_own_ref, ...), custom_call_target="tpu_custom_call" | custom-call | tf_op jit(solution)/shard_map/pallas_call | solution.py:23
  55.3 1.9 %collective-permute-start.6 = (bf16[2,48,1536]{2,1,0:T(8,128)(2,1)}, bf16[2,48,1536]{2,1,0:T(8,128)(2,1)S(1)}, u32[]{:S(2)}, u32[]{:S(2)}) collective-permute-start(bf16[2,48,1536]{2,1,0:T(8,128)(2,1)} %get-tuple-element.26), channel_id=1, source_target_pairs={{0,4},{4,0},{8,12},{12,8},{16,20},{20,16},{24,28},{28,24},{1,5},{5... | collective-permute-start | bytes 884744 | tf_op jit(solution)/shard_map/ppermute | solution.py:36
  57.3 7.7 %collective-permute-done.6 = bf16[2,48,1536]{2,1,0:T(8,128)(2,1)S(1)} collective-permute-done((bf16[2,48,1536]{2,1,0:T(8,128)(2,1)}, bf16[2,48,1536]{2,1,0:T(8,128)(2,1)S(1)}, u32[]{:S(2)}, u32[]{:S(2)}) %collective-permute-start.6) | collective-permute-done | bytes 294944 | tf_op jit(solution)/shard_map/ppermute | solution.py:36
  64.9 2.0 %convert_add_fusion.2 = f32[2,48,1536]{2,1,0:T(8,128)} fusion(f32[2,48,1536]{2,1,0:T(8,128)} %get-tuple-element.25, bf16[2,48,1536]{2,1,0:T(8,128)(2,1)S(1)} %collective-permute-done.6), kind=kLoop, calls=%fused_computation.14 | loop fusion | flops 294912 | bytes 1474560 | tf_op jit(solution)/shard_map/add | solution.py:193
  75.3 3.7 %collective-permute-start.8 = (bf16[48,1536]{1,0:T(8,128)(2,1)S(1)}, bf16[48,1536]{1,0:T(8,128)(2,1)}, u32[]{:S(2)}, u32[]{:S(2)}) collective-permute-start(bf16[48,1536]{1,0:T(8,128)(2,1)S(1)} %fusion.8), channel_id=1, source_target_pairs={{0,24},{4,28},{8,16},{12,20},{16,8},{20,12},{24,0},{28,4},{1,25},{... | collective-permute-start | bytes 442376 | tf_op jit(solution)/shard_map/ppermute | solution.py:36
  80.1 7.5 %shard_map.116 = (f32[2,64,768]{2,1,0:T(8,128)}, bf16[2,64,768]{2,1,0:T(8,128)(2,1)}) custom-call(s32[1]{0:T(128)} %bitcast.12.flip_ref.fc_ref, bf16[1152,512]{1,0:T(8,128)(2,1)} %get-tuple-element.24.gp_ref.gp_own_ref, bf16[1152,512]{1,0:T(8,128)(2,1)} %collective-permute-done.11.gp_ref.gp_other_ref, bf16[768,1152]{1,0:T(8,128)(2,1)} %get-tuple-element.42.w_own_ref, ...), custom_call_target="tpu_custom_call" | custom-call | tf_op jit(solution)/shard_map/pallas_call | solution.py:23
  88.8 3.3 %shard_map.115 = (f32[2,48,1536]{2,1,0:T(8,128)}, bf16[2,48,1536]{2,1,0:T(8,128)(2,1)}) custom-call(s32[1]{0:T(128)} %bitcast.13.share_ref, s32[1]{0:T(128)} %bitcast.11.flip_ref.fb_ref, bf16[768,512]{1,0:T(8,128)(2,1)} %get-tuple-element.23.normed_ref, bf16[1152,512]{1,0:T(8,128)(2,1)} %collective-permute-done.11.gp_ref.gp_other_ref, ...), custom_call_target="tpu_custom_call" | custom-call | tf_op jit(solution)/shard_map/pallas_call | solution.py:23
  92.0 2.0 %collective-permute-start.12 = (bf16[2,48,1536]{2,1,0:T(8,128)(2,1)}, bf16[2,48,1536]{2,1,0:T(8,128)(2,1)S(1)}, u32[]{:S(2)}, u32[]{:S(2)}) collective-permute-start(bf16[2,48,1536]{2,1,0:T(8,128)(2,1)} %get-tuple-element.28), channel_id=1, source_target_pairs={{0,8},{4,12},{8,0},{12,4},{16,24},{20,28},{24,16},{28,20},{1,9},{5... | collective-permute-start | bytes 884744 | tf_op jit(solution)/shard_map/ppermute | solution.py:36
  94.0 2.3 %collective-permute-done.17 = bf16[2,64,768]{2,1,0:T(8,128)(2,1)S(1)} collective-permute-done((bf16[2,64,768]{2,1,0:T(8,128)(2,1)}, bf16[2,64,768]{2,1,0:T(8,128)(2,1)S(1)}, u32[]{:S(2)}, u32[]{:S(2)}) %collective-permute-start.17) | collective-permute-done | bytes 196640 | tf_op jit(solution)/shard_map/ppermute | solution.py:36
  98.0 5.7 %collective-permute-done.12 = bf16[2,48,1536]{2,1,0:T(8,128)(2,1)S(1)} collective-permute-done((bf16[2,48,1536]{2,1,0:T(8,128)(2,1)}, bf16[2,48,1536]{2,1,0:T(8,128)(2,1)S(1)}, u32[]{:S(2)}, u32[]{:S(2)}) %collective-permute-start.12) | collective-permute-done | bytes 294944 | tf_op jit(solution)/shard_map/ppermute | solution.py:36
  106.7 6.4 %collective-permute-done.13 = bf16[48,1536]{1,0:T(8,128)(2,1)S(1)} collective-permute-done((bf16[48,1536]{1,0:T(8,128)(2,1)S(1)}, bf16[48,1536]{1,0:T(8,128)(2,1)S(1)}, u32[]{:S(2)}, u32[]{:S(2)}) %collective-permute-start.13) | collective-permute-done | bytes 147488 | tf_op jit(solution)/shard_map/ppermute | solution.py:36
  115.3 3.3 %collective-permute-done.14 = bf16[48,1536]{1,0:T(8,128)(2,1)S(1)} collective-permute-done((bf16[48,1536]{1,0:T(8,128)(2,1)S(1)}, bf16[48,1536]{1,0:T(8,128)(2,1)S(1)}, u32[]{:S(2)}, u32[]{:S(2)}) %collective-permute-start.14) | collective-permute-done | bytes 147488 | tf_op jit(solution)/shard_map/ppermute | solution.py:36
  121.3 3.3 %collective-permute-start.21 = (bf16[2,64,768]{2,1,0:T(8,128)(2,1)S(1)}, bf16[2,64,768]{2,1,0:T(8,128)(2,1)S(1)}, u32[]{:S(2)}, u32[]{:S(2)}) collective-permute-start(bf16[2,64,768]{2,1,0:T(8,128)(2,1)S(1)} %pad_maximum_fusion.5), channel_id=1, source_target_pairs={{0,24},{4,28},{8,16},{12,20},{16,8},{20,12},{24,0},{28,4},{1,25},{... | collective-permute-start | bytes 589832 | tf_op jit(solution)/shard_map/ppermute | solution.py:36
  124.6 2.6 %collective-permute-done.15.b1 = bf16[48,1536]{1,0:T(8,128)(2,1)S(1)} collective-permute-done((bf16[48,1536]{1,0:T(8,128)(2,1)S(1)}, bf16[48,1536]{1,0:T(8,128)(2,1)S(1)}, u32[]{:S(2)}, u32[]{:S(2)}) %collective-permute-start.15) | collective-permute-done | bytes 147488 | tf_op jit(solution)/shard_map/ppermute | solution.py:36
  128.4 2.0 %fusion.2 = bf16[1,128,768]{2,1,0:T(8,128)(2,1)} fusion(f32[128,768]{1,0:T(8,128)S(1)} %fusion.9, bf16[768,768]{1,0:T(8,128)(2,1)S(1)} %copy-done, bf16[768,512]{1,0:T(8,128)(2,1)} %bitcast.62, s32[]{:T(128)S(6)} %select_n.150, f32[128]{0:T(128)S(1)} %copy-done.30), kind=kOutput, calls=%fused_computation.7 | convolution fusion | flops 151289856 | bytes 1966596 | tf_op jit(solution)/shard_map/dot_general | solution.py:19
  130.4 3.6 %collective-permute-done.16.b2 = bf16[2,48,1536]{2,1,0:T(8,128)(2,1)S(1)} collective-permute-done((bf16[2,48,1536]{2,1,0:T(8,128)(2,1)S(1)}, bf16[2,48,1536]{2,1,0:T(8,128)(2,1)S(1)}, u32[]{:S(2)}, u32[]{:S(2)}) %collective-permute-start.16) | collective-permute-done | bytes 294944 | tf_op jit(solution)/shard_map/ppermute | solution.py:36
  134.8 3.2 %shard_map.117 = (f32[256,768]{1,0:T(8,128)}, f32[192,2304]{1,0:T(8,128)}, f32[192,768]{1,0:T(8,128)}) custom-call(s32[1]{0:T(128)} %bitcast.1.refs_0_.core_ref, s32[1]{0:T(128)} %bitcast.10.flip_ref.fa_ref, s32[1]{0:T(128)} %bitcast.11.flip_ref.fb_ref, s32[1]{0:T(128)} %bitcast.12.flip_ref.fc_ref, bf16[48,1536]{1,0:T(8,128)(2,1)} %copy-done.16, ...), custom_call_target="tpu_custom_call" | custom-call | tf_op jit(solution)/shard_map/pallas_call | solution.py:23
  (133 shorter events, 40.7 us)
Async XLA Ops:
  0.6 30.0 %copy-start = (bf16[768,768]{1,0:T(8,128)(2,1)S(1)}, bf16[768,768]{1,0:T(8,128)(2,1)}, u32[]{:S(2)}) copy-start(bf16[768,768]{1,0:T(8,128)(2,1)} %param.14) | copy-start | bytes 3538948
  6.9 6.5 %collective-permute-start = (bf16[256,1024]{1,0:T(8,128)(2,1)}, bf16[256,1024]{1,0:T(8,128)(2,1)S(1)}, u32[]{:S(2)}, u32[]{:S(2)}) collective-permute-start(bf16[256,1024]{1,0:T(8,128)(2,1)} %get-tuple-element.21), channel_id=1, source_target_pairs={{0,1},{1,0},{2,3},{3,2},{4,5},{5,4},{6,7},{7,6},{8,9},{9,8},{10,11... | collective-permute-start | bytes 1572872 | tf_op jit(solution)/shard_map/ppermute | solution.py:36
  7.4 17.2 %collective-permute-start.3 = (bf16[1,128,768]{2,1,0:T(8,128)(2,1)}, bf16[1,128,768]{2,1,0:T(8,128)(2,1)}, u32[]{:S(2)}, u32[]{:S(2)}) collective-permute-start(bf16[1,128,768]{2,1,0:T(8,128)(2,1)} %param.15), channel_id=1, source_target_pairs={{0,2},{1,3},{2,0},{3,1},{4,6},{5,7},{6,4},{7,5},{8,10},{9,11},{10,... | collective-permute-start | bytes 589832 | tf_op jit(solution)/shard_map/ppermute | solution.py:36
  14.4 14.3 %collective-permute-start.1 = (bf16[256,1024]{1,0:T(8,128)(2,1)}, bf16[256,1024]{1,0:T(8,128)(2,1)}, u32[]{:S(2)}, u32[]{:S(2)}) collective-permute-start(bf16[256,1024]{1,0:T(8,128)(2,1)} %fusion.3), channel_id=1, source_target_pairs={{0,2},{1,3},{2,0},{3,1},{4,6},{5,7},{6,4},{7,5},{8,10},{9,11},{10,... | collective-permute-start | bytes 1572872 | tf_op jit(solution)/shard_map/ppermute | solution.py:36
  28.4 1.9 %collective-permute-start.4 = (bf16[256,768]{0,1:T(8,128)(2,1)}, bf16[256,768]{0,1:T(8,128)(2,1)S(1)}, u32[]{:S(2)}, u32[]{:S(2)}) collective-permute-start(bf16[256,768]{0,1:T(8,128)(2,1)} %copy.26), channel_id=1, source_target_pairs={{0,1},{1,0},{2,3},{3,2},{4,5},{5,4},{6,7},{7,6},{8,9},{9,8},{10,11... | collective-permute-start | bytes 1179656 | tf_op jit(solution)/shard_map/ppermute | solution.py:36
  30.0 2.0 %collective-permute-start.2 = (bf16[256,1024]{1,0:T(8,128)(2,1)S(1)}, bf16[256,1024]{1,0:T(8,128)(2,1)S(1)}, u32[]{:S(2)}, u32[]{:S(2)}) collective-permute-start(bf16[256,1024]{1,0:T(8,128)(2,1)S(1)} %divide_convert_fusion.refs_2_), channel_id=1, source_target_pairs={{0,1},{1,0},{2,3},{3,2},{4,5},{5,4},{6,7},{7,6},{8,9},{9,8},{10,11... | collective-permute-start | bytes 1572872 | tf_op jit(solution)/shard_map/ppermute | solution.py:36
  47.1 2.1 %collective-permute-start.5 = (bf16[384,512]{1,0:T(8,128)(2,1)}, bf16[384,512]{1,0:T(8,128)(2,1)}, u32[]{:S(2)}, u32[]{:S(2)}) collective-permute-start(bf16[384,512]{1,0:T(8,128)(2,1)} %get-tuple-element.22), channel_id=1, source_target_pairs={{0,1},{1,0},{2,3},{3,2},{4,5},{5,4},{6,7},{7,6},{8,9},{9,8},{10,11... | collective-permute-start | bytes 1179656 | tf_op jit(solution)/shard_map/ppermute | solution.py:36
  55.3 9.6 %collective-permute-start.6 = (bf16[2,48,1536]{2,1,0:T(8,128)(2,1)}, bf16[2,48,1536]{2,1,0:T(8,128)(2,1)S(1)}, u32[]{:S(2)}, u32[]{:S(2)}) collective-permute-start(bf16[2,48,1536]{2,1,0:T(8,128)(2,1)} %get-tuple-element.26), channel_id=1, source_target_pairs={{0,4},{4,0},{8,12},{12,8},{16,20},{20,16},{24,28},{28,24},{1,5},{5... | collective-permute-start | bytes 884744 | tf_op jit(solution)/shard_map/ppermute | solution.py:36
  57.2 22.8 %collective-permute-start.11 = (bf16[1152,512]{1,0:T(8,128)(2,1)S(1)}, bf16[1152,512]{1,0:T(8,128)(2,1)}, u32[]{:S(2)}, u32[]{:S(2)}) collective-permute-start(bf16[1152,512]{1,0:T(8,128)(2,1)S(1)} %copy-done.5), channel_id=1, source_target_pairs={{0,1},{1,0},{2,3},{3,2},{4,5},{5,4},{6,7},{7,6},{8,9},{9,8},{10,11... | collective-permute-start | bytes 3538952 | tf_op jit(solution)/shard_map/ppermute | solution.py:36
  68.5 5.8 %collective-permute-start.7 = (bf16[48,1536]{1,0:T(8,128)(2,1)}, bf16[48,1536]{1,0:T(8,128)(2,1)}, u32[]{:S(2)}, u32[]{:S(2)}) collective-permute-start(bf16[48,1536]{1,0:T(8,128)(2,1)} %fusion.14), channel_id=1, source_target_pairs={{0,8},{4,12},{8,0},{12,4},{16,24},{20,28},{24,16},{28,20},{1,9},{5... | collective-permute-start | bytes 442376 | tf_op jit(solution)/shard_map/ppermute | solution.py:36
  75.3 12.4 %collective-permute-start.8 = (bf16[48,1536]{1,0:T(8,128)(2,1)S(1)}, bf16[48,1536]{1,0:T(8,128)(2,1)}, u32[]{:S(2)}, u32[]{:S(2)}) collective-permute-start(bf16[48,1536]{1,0:T(8,128)(2,1)S(1)} %fusion.8), channel_id=1, source_target_pairs={{0,24},{4,28},{8,16},{12,20},{16,8},{20,12},{24,0},{28,4},{1,25},{... | collective-permute-start | bytes 442376 | tf_op jit(solution)/shard_map/ppermute | solution.py:36
  87.5 8.9 %collective-permute-start.17 = (bf16[2,64,768]{2,1,0:T(8,128)(2,1)}, bf16[2,64,768]{2,1,0:T(8,128)(2,1)S(1)}, u32[]{:S(2)}, u32[]{:S(2)}) collective-permute-start(bf16[2,64,768]{2,1,0:T(8,128)(2,1)} %get-tuple-element.32), channel_id=1, source_target_pairs={{0,24},{4,28},{8,16},{12,20},{16,8},{20,12},{24,0},{28,4},{1,25},{... | collective-permute-start | bytes 589832 | tf_op jit(solution)/shard_map/ppermute | solution.py:36
  88.7 30.9 %copy-start.16 = (bf16[48,1536]{1,0:T(8,128)(2,1)}, bf16[48,1536]{1,0:T(8,128)(2,1)S(1)}, u32[]{:S(2)}) copy-start(bf16[48,1536]{1,0:T(8,128)(2,1)S(1)} %add_convert_fusion.1.a0) | copy-start | bytes 442372
  88.7 30.9 %collective-permute-start.9 = (bf16[48,1536]{1,0:T(8,128)(2,1)S(1)}, bf16[48,1536]{1,0:T(8,128)(2,1)S(1)}, u32[]{:S(2)}, u32[]{:S(2)}) collective-permute-start(bf16[48,1536]{1,0:T(8,128)(2,1)S(1)} %add_convert_fusion.1.a0), channel_id=1, source_target_pairs={{0,8},{4,12},{8,0},{12,4},{16,24},{20,28},{24,16},{28,20},{1,9},{5... | collective-permute-start | bytes 442376 | tf_op jit(solution)/shard_map/ppermute | solution.py:36
  92.0 11.6 %collective-permute-start.12 = (bf16[2,48,1536]{2,1,0:T(8,128)(2,1)}, bf16[2,48,1536]{2,1,0:T(8,128)(2,1)S(1)}, u32[]{:S(2)}, u32[]{:S(2)}) collective-permute-start(bf16[2,48,1536]{2,1,0:T(8,128)(2,1)} %get-tuple-element.28), channel_id=1, source_target_pairs={{0,8},{4,12},{8,0},{12,4},{16,24},{20,28},{24,16},{28,20},{1,9},{5... | collective-permute-start | bytes 884744 | tf_op jit(solution)/shard_map/ppermute | solution.py:36
  96.4 9.8 %collective-permute-start.18 = (bf16[64,768]{1,0:T(8,128)(2,1)S(1)}, bf16[64,768]{1,0:T(8,128)(2,1)S(1)}, u32[]{:S(2)}, u32[]{:S(2)}) collective-permute-start(bf16[64,768]{1,0:T(8,128)(2,1)S(1)} %fusion.16), channel_id=1, source_target_pairs={{0,4},{4,0},{8,12},{12,8},{16,20},{20,16},{24,28},{28,24},{1,5},{5... | collective-permute-start | bytes 294920 | tf_op jit(solution)/shard_map/ppermute | solution.py:36
  104.8 8.3 %collective-permute-start.13 = (bf16[48,1536]{1,0:T(8,128)(2,1)S(1)}, bf16[48,1536]{1,0:T(8,128)(2,1)S(1)}, u32[]{:S(2)}, u32[]{:S(2)}) collective-permute-start(bf16[48,1536]{1,0:T(8,128)(2,1)S(1)} %fusion.15), channel_id=1, source_target_pairs={{0,24},{4,28},{8,16},{12,20},{16,8},{20,12},{24,0},{28,4},{1,25},{... | collective-permute-start | bytes 442376 | tf_op jit(solution)/shard_map/ppermute | solution.py:36
  106.3 8.4 %collective-permute-start.19 = (bf16[64,768]{1,0:T(8,128)(2,1)S(1)}, bf16[64,768]{1,0:T(8,128)(2,1)S(1)}, u32[]{:S(2)}, u32[]{:S(2)}) collective-permute-start(bf16[64,768]{1,0:T(8,128)(2,1)S(1)} %fusion.12), channel_id=1, source_target_pairs={{0,8},{4,12},{8,0},{12,4},{16,24},{20,28},{24,16},{28,20},{1,9},{5... | collective-permute-start | bytes 294920 | tf_op jit(solution)/shard_map/ppermute | solution.py:36
  113.1 5.5 %collective-permute-start.14 = (bf16[48,1536]{1,0:T(8,128)(2,1)S(1)}, bf16[48,1536]{1,0:T(8,128)(2,1)S(1)}, u32[]{:S(2)}, u32[]{:S(2)}) collective-permute-start(bf16[48,1536]{1,0:T(8,128)(2,1)S(1)} %fusion.6), channel_id=1, source_target_pairs={{0,4},{4,0},{8,12},{12,8},{16,20},{20,16},{24,28},{28,24},{1,5},{5... | collective-permute-start | bytes 442376 | tf_op jit(solution)/shard_map/ppermute | solution.py:36
  114.8 6.5 %collective-permute-start.20 = (bf16[64,768]{1,0:T(8,128)(2,1)S(1)}, bf16[64,768]{1,0:T(8,128)(2,1)S(1)}, u32[]{:S(2)}, u32[]{:S(2)}) collective-permute-start(bf16[64,768]{1,0:T(8,128)(2,1)S(1)} %add_convert_fusion.2.c0), channel_id=1, source_target_pairs={{0,4},{4,0},{8,12},{12,8},{16,20},{20,16},{24,28},{28,24},{1,5},{5... | collective-permute-start | bytes 294920 | tf_op jit(solution)/shard_map/ppermute | solution.py:36
  118.6 8.6 %collective-permute-start.15 = (bf16[48,1536]{1,0:T(8,128)(2,1)S(1)}, bf16[48,1536]{1,0:T(8,128)(2,1)S(1)}, u32[]{:S(2)}, u32[]{:S(2)}) collective-permute-start(bf16[48,1536]{1,0:T(8,128)(2,1)S(1)} %add_convert_fusion.b0), channel_id=1, source_target_pairs={{0,24},{4,28},{8,16},{12,20},{16,8},{20,12},{24,0},{28,4},{1,25},{... | collective-permute-start | bytes 442376 | tf_op jit(solution)/shard_map/ppermute | solution.py:36
  119.7 10.7 %collective-permute-start.10 = (bf16[2,48,1536]{2,1,0:T(8,128)(2,1)S(1)}, bf16[2,48,1536]{2,1,0:T(8,128)(2,1)S(1)}, u32[]{:S(2)}, u32[]{:S(2)}) collective-permute-start(bf16[2,48,1536]{2,1,0:T(8,128)(2,1)S(1)} %pad_maximum_fusion.3), channel_id=1, source_target_pairs={{0,4},{4,0},{8,12},{12,8},{16,20},{20,16},{24,28},{28,24},{1,5},{5... | collective-permute-start | bytes 884744 | tf_op jit(solution)/shard_map/ppermute | solution.py:36
  121.3 9.1 %collective-permute-start.21 = (bf16[2,64,768]{2,1,0:T(8,128)(2,1)S(1)}, bf16[2,64,768]{2,1,0:T(8,128)(2,1)S(1)}, u32[]{:S(2)}, u32[]{:S(2)}) collective-permute-start(bf16[2,64,768]{2,1,0:T(8,128)(2,1)S(1)} %pad_maximum_fusion.5), channel_id=1, source_target_pairs={{0,24},{4,28},{8,16},{12,20},{16,8},{20,12},{24,0},{28,4},{1,25},{... | collective-permute-start | bytes 589832 | tf_op jit(solution)/shard_map/ppermute | solution.py:36
  127.3 6.8 %collective-permute-start.16 = (bf16[2,48,1536]{2,1,0:T(8,128)(2,1)S(1)}, bf16[2,48,1536]{2,1,0:T(8,128)(2,1)S(1)}, u32[]{:S(2)}, u32[]{:S(2)}) collective-permute-start(bf16[2,48,1536]{2,1,0:T(8,128)(2,1)S(1)} %pad_maximum_fusion.4), channel_id=1, source_target_pairs={{0,8},{4,12},{8,0},{12,4},{16,24},{20,28},{24,16},{28,20},{1,9},{5... | collective-permute-start | bytes 884744 | tf_op jit(solution)/shard_map/ppermute | solution.py:36
  (29 other events, 195.3 us)
